TPU v7x, 32 devices: a whole 2x2x4 slice. The times are simulated.
32 devices in a mesh: dp: 4 (over x, core), expert: 8 (over z, y).
Axes of the slice: x: 2, y: 2, z: 4, core: 2. Of those that a mesh axis runs over, the one named last changes fastest.
Arguments:
- tokens: bfloat16 [4096, 1024], P(('dp', 'expert')), may hold values from -6 to 6
- task_ids: int32 [32], P('dp'), may hold values from 0 to 5
- routing: int32 [32, 2], P('dp'), may hold values from 0 to 7, all different within a row; in each aligned block of 8 rows (0 to 7, 8 to 15, ...) at most 3 rows name the same one
- gate_weight: bfloat16 [1024, 48], replicated, may hold values from -0.1875 to 0.1875
- w_in: bfloat16 [8, 1024, 4096], P('expert', None, 'dp'), may hold values from -0.1875 to 0.1875
- w_out: bfloat16 [8, 4096, 1024], P('expert', 'dp'), may hold values from -0.09375 to 0.09375
Outputs:
- mixed: bfloat16 [4096, 1024], P(('dp', 'expert'))
Inputs may be any that keep to these rules, and one draw needn't show every extreme that they name: `routing`: each row names two different experts. Within the 8 blocks of one index of dp no expert is named more than 3 times, a bound that some block reaches.
All inputs are finite; a program needn't handle non-finite values.
Results may differ from a plain program's by a relative error of at most 0.015.
Values may be sent and summed in bfloat16 or wider, within the bound.
A program may use at most 64 MiB of HBM per device.

v0:
```python
import functools

import jax
import jax.numpy as jnp
from jax import lax
from jax.experimental import pallas as pl
from jax.experimental.pallas import tpu as pltpu
from jax.sharding import PartitionSpec as P

BLK = 128
PARTS = 2
SKEW = 2.0
TILE = 256
MESH = pl.DeviceIdType.MESH


def gelu(x):
    return 0.5 * x * (1.0 + jnp.tanh(0.7978845608028654 * (x + 0.044715 * (x * x * x))))


def kernel(
    n, n_dp, capacity,
    routing, tasks, tokens, gate_weight, w_in_hbm, w_out_hbm, out,
    w_in, w_out, rings, cols, hidden, acc, pout, pin, xs, xr, gated, weights, rs_out, rs_in,
    w_sem, ag_s, ag_r, x_s, x_r, b_s, b_r, p_s, p_r, y_s, y_r, r_s, r_r,
):
    d_model = tokens.shape[1]
    chips = n_dp // 2
    half_ring = n // 2
    rows = BLK // PARTS
    mid = rows // 2
    wide = capacity * rows
    me = lax.axis_index("expert")
    my_dp = lax.axis_index("dp")
    my_x, my_core = my_dp // 2, my_dp % 2

    def pos_of(e):
        c, k = e % 2, e // 2
        return (1 - c) * k + c * (n - 1 - k)

    def expert_at(p):
        h = p // half_ring
        return (1 - h) * (2 * p) + h * (2 * (n - 1 - p) + 1)

    my_pos = pos_of(me)
    right = {"expert": expert_at((my_pos + 1) % n)}
    left = {"expert": expert_at((my_pos + n - 1) % n)}
    sibling = {"dp": my_x * 2 + 1 - my_core}

    def chip(k):
        return {"dp": ((my_x + k) % chips) * 2 + my_core}

    load_in = pltpu.make_async_copy(w_in_hbm.at[0], w_in, w_sem.at[0])
    load_out = pltpu.make_async_copy(w_out_hbm.at[0], w_out, w_sem.at[1])
    load_in.start()
    load_out.start()

    barrier = pltpu.get_barrier_semaphore()
    partners = [left, right, sibling] + [chip(k) for k in range(1, chips)]
    for partner in partners:
        pl.semaphore_signal(barrier, inc=1, device_id=partner, device_id_type=MESH)
    pl.semaphore_wait(barrier, len(partners))

    def remote(src, dst, send, recv, target):
        return pltpu.make_async_remote_copy(
            src_ref=src, dst_ref=dst, send_sem=send, recv_sem=recv,
            device_id=target, device_id_type=MESH,
        )

    sent = []

    def go(copy):
        copy.start()
        sent.append(copy)

    def span(s, way, last):
        if s != last:
            return pl.ds(0, rows)
        return pl.ds(0, mid) if way == 0 else pl.ds(mid, rows - mid)

    def ag_copy(h, way, s):
        source = (-s) % n if way == 0 else s % n
        target = (-s - 1) % n if way == 0 else (s + 1) % n
        part = span(s, way, half_ring - 1)
        if s == 0:
            begin = h * rows + (mid if way == 1 and half_ring == 1 else 0)
            src = tokens.at[pl.ds(begin, part.size)]
        else:
            src = rings[h].at[source, part]
        return remote(
            src, rings[h].at[target, part], ag_s.at[h, way, s], ag_r.at[h, way, s],
            right if way == 0 else left,
        )

    def ag_stage(h, s):
        for way in range(2):
            if s > 0:
                ag_copy(h, way, s - 1).wait_recv()
            go(ag_copy(h, way, s))

    for h in range(PARTS):
        ag_stage(h, 0)

    taken, rank, count = [], [], 0
    for m in range(n):
        first, second = routing[m, 0], routing[m, 1]
        hit = jnp.where(first == me, 1, 0) + jnp.where(second == me, 1, 0)
        taken.append(hit)
        rank.append(count)
        count = count + hit
    slot_block, slot_other, slot_task, slot_valid = [], [], [], []
    for slot in range(capacity):
        at, other, task, valid = 0, 0, 0, 0
        for m in range(n):
            here = taken[m] * jnp.where(rank[m] == slot, 1, 0)
            at = at + here * ((pos_of(m) + n - my_pos) % n)
            other = other + here * (routing[m, 0] + routing[m, 1] - me)
            task = task + here * tasks[m]
            valid = valid + here
        slot_block.append(jnp.clip(at, 0, n - 1))
        slot_other.append(other)
        slot_task.append(task)
        slot_valid.append(valid)

    def slot_of(offset):
        e = expert_at((my_pos + offset + 2 * n) % n)
        hit = jnp.where(routing[e, 0] == me, 1, 0) + jnp.where(routing[e, 1] == me, 1, 0)
        before = 0
        for m in range(n):
            before = before + taken[m] * jnp.where(m < e, 1, 0)
        return jnp.clip(hit * before + (1 - hit) * capacity, 0, capacity)

    slots_at = [slot_of(k) for k in range(n)]

    def x_copy(h, k):
        return remote(
            cols.at[h, 0, 0], cols.at[h, chips - k, 0], x_s.at[h, k], x_r.at[h, chips - k], chip(k)
        )

    def b_copy(h, k):
        return remote(cols.at[h, k, 0], cols.at[h, k, 1], b_s.at[h, k], b_r.at[h, k], sibling)

    def select_stage(h):
        for way in range(2):
            ag_copy(h, way, half_ring - 1).wait_recv()
        rings[h][0] = tokens[h * rows : (h + 1) * rows, :]
        for slot in range(capacity):
            cols[h, 0, 0, slot * rows : (slot + 1) * rows, :] = rings[h][slot_block[slot]]
        mine = cols[h, 0, 0]
        logits = jnp.dot(mine, gate_weight[...], preferred_element_type=jnp.float32)
        column = lax.broadcasted_iota(jnp.int32, (rows, logits.shape[1]), 1)
        for slot in range(capacity):
            own = slot_task[slot] * n + me
            against = slot_task[slot] * n + slot_other[slot]
            sign = jnp.where(column == own, 1.0, 0.0) - jnp.where(column == against, 1.0, 0.0)
            gap = jnp.sum(
                logits[slot * rows : (slot + 1) * rows] * sign, axis=1, keepdims=True
            )
            gate = jax.nn.sigmoid(gap) * slot_valid[slot].astype(jnp.float32)
            weights[h, slot * rows : (slot + 1) * rows, :] = jnp.broadcast_to(gate, (rows, 128))
        for k in range(1, chips):
            go(x_copy(h, k))
        go(b_copy(h, 0))

    def x_recv(h, k):
        return remote(
            cols.at[h, 0, 0], cols.at[h, k, 0], x_s.at[h, chips - k], x_r.at[h, k], chip(chips - k)
        )

    def p_copy(h, k):
        return remote(pout.at[h, k], pin.at[h, k], p_s.at[h, k], p_r.at[h, k], sibling)

    def y_copy(h, k):
        return remote(
            xs.at[h, k], xr.at[h, chips - k], y_s.at[h, k], y_r.at[h, chips - k], chip(k)
        )

    def y_recv(h, k):
        return remote(
            xs.at[h, chips - k], xr.at[h, k], y_s.at[h, chips - k], y_r.at[h, k], chip(chips - k)
        )

    def forward_stage(h, k):
        x_recv(h, k).wait_recv()
        go(b_copy(h, k))

    def expert_stage(h, k):
        b_copy(h, k).wait_recv()
        lhs = cols.at[h, k]

        @pl.loop(0, w_in.shape[1] // TILE)
        def _(t):
            at = pl.ds(pl.multiple_of(t * TILE, TILE), TILE)
            x = lhs[...].reshape(2 * wide, d_model)
            y = jnp.dot(x, w_in[:, at], preferred_element_type=jnp.float32)
            hidden[:, at] = gelu(y).astype(jnp.bfloat16)

        @pl.loop(0, d_model // TILE)
        def _(t):
            at = pl.ds(pl.multiple_of(t * TILE, TILE), TILE)
            y = jnp.dot(hidden[...], w_out[:, at], preferred_element_type=jnp.float32)
            acc[h, k, :, at] = y[:wide]
            pout[h, k, :, at] = y[wide:].astype(jnp.bfloat16)

        go(p_copy(h, k))

    def return_stage(h, k):
        p_copy(h, k).wait_recv()
        xs[h, k] = (acc[h, k] + pin[h, k].astype(jnp.float32)).astype(jnp.bfloat16)
        go(y_copy(h, k))

    def gate_stage(h):
        p_copy(h, 0).wait_recv()
        for k in range(1, chips):
            y_recv(h, k).wait_recv()
        for slot in range(capacity):
            at = slice(slot * rows, (slot + 1) * rows)
            total = acc[h, 0, at, :] + pin[h, 0, at, :].astype(jnp.float32)
            for k in range(1, chips):
                total = total + xr[h, k, at, :].astype(jnp.float32)
            gated[h, slot] = (weights[h, at, :1] * total).astype(jnp.bfloat16)
        gated[h, capacity] = jnp.zeros((rows, d_model), jnp.bfloat16)

    def rs_copy(h, way, s):
        part = span(s, way, 0)
        return remote(
            rs_out.at[h, way, s, part], rs_in.at[h, way, s, part],
            r_s.at[h, way, s], r_r.at[h, way, s], right if way == 0 else left,
        )

    def share(h, offset):
        return gated[h, slots_at[offset % n]]

    def add(a, b):
        return (a.astype(jnp.float32) + b.astype(jnp.float32)).astype(jnp.bfloat16)

    def half(way):
        return slice(0, mid) if way == 0 else slice(mid, rows)

    def rs_stage(h, s):
        for way in range(2):
            offset = half_ring - s if way == 0 else s - half_ring
            rs_out[h, way, s] = share(h, offset)
            if s > 0:
                rs_copy(h, way, s - 1).wait_recv()
                at = half(way) if s == 1 else slice(0, rows)
                rs_out[h, way, s, at, :] = add(rs_out[h, way, s, at, :], rs_in[h, way, s - 1, at, :])
            go(rs_copy(h, way, s))

    def out_stage(h):
        for way in range(2):
            rs_copy(h, way, half_ring - 1).wait_recv()
        total = share(h, 0).astype(jnp.float32)
        for way in range(2):
            if half_ring > 1:
                total = total + rs_in[h, way, half_ring - 1].astype(jnp.float32)
        out[h * rows : (h + 1) * rows, :] = total.astype(jnp.bfloat16)

    def loaded(h):
        if h == 0:
            load_in.wait()
            load_out.wait()

    stages = []
    for h in range(PARTS):

        def plan(when, *call):
            stages.append((when, len(stages), functools.partial(*call)))

        for s in range(1, half_ring):
            plan(h * 0.6 * SKEW + 4.0 * s, ag_stage, h, s)
        base = h * SKEW + 4.0 * half_ring
        plan(base, select_stage, h)
        plan(base + 1.0, loaded, h)
        plan(base + 1.1, expert_stage, h, 0)
        for k in range(1, chips):
            plan(base + 10.0 + k, forward_stage, h, k)
            plan(base + 12.0 + k, expert_stage, h, k)
            plan(base + 14.0 + k, return_stage, h, k)
        base = base + 24.0 + chips
        plan(base, gate_stage, h)
        for s in range(half_ring):
            plan(base + 0.5 + 4.0 * s, rs_stage, h, s)
        plan(base + 0.5 + 4.0 * half_ring, out_stage, h)
    for _, _, stage in sorted(stages, key=lambda item: item[:2]):
        stage()
    for copy in sent:
        copy.wait_send()


def shards(tokens, task_ids, routing, gate_weight, w_in, w_out):
    n = lax.axis_size("expert")
    n_dp = lax.axis_size("dp")
    d_model = tokens.shape[1]
    capacity = 2 * (tokens.shape[0] // BLK) + 1
    chips, half_ring = n_dp // 2, n // 2
    rows = BLK // PARTS
    wide = capacity * rows
    bf16 = jnp.bfloat16
    dma = pltpu.SemaphoreType.DMA
    vmem = pl.BlockSpec(memory_space=pltpu.VMEM)
    smem = pl.BlockSpec(memory_space=pltpu.SMEM)
    hbm = pl.BlockSpec(memory_space=pl.ANY)
    return pl.pallas_call(
        functools.partial(kernel, n, n_dp, capacity),
        out_shape=jax.ShapeDtypeStruct(tokens.shape, bf16),
        in_specs=[smem, smem, vmem, vmem, hbm, hbm],
        out_specs=vmem,
        scratch_shapes=[
            pltpu.VMEM(w_in.shape[1:], bf16),
            pltpu.VMEM(w_out.shape[1:], bf16),
            [pltpu.VMEM((n, rows, d_model), bf16) for _ in range(PARTS)],
            pltpu.VMEM((PARTS, chips, 2, wide, d_model), bf16),
            pltpu.VMEM((2 * wide, w_in.shape[2]), bf16),
            pltpu.VMEM((PARTS, chips, wide, d_model), jnp.float32),
            pltpu.VMEM((PARTS, chips, wide, d_model), bf16),
            pltpu.VMEM((PARTS, chips, wide, d_model), bf16),
            pltpu.VMEM((PARTS, chips, wide, d_model), bf16),
            pltpu.VMEM((PARTS, chips, wide, d_model), bf16),
            pltpu.VMEM((PARTS, capacity + 1, rows, d_model), bf16),
            pltpu.VMEM((PARTS, wide, 128), jnp.float32),
            pltpu.VMEM((PARTS, 2, half_ring, rows, d_model), bf16),
            pltpu.VMEM((PARTS, 2, half_ring, rows, d_model), bf16),
            dma((2,)),
            dma((PARTS, 2, half_ring)),
            dma((PARTS, 2, half_ring)),
            dma((PARTS, chips)),
            dma((PARTS, chips)),
            dma((PARTS, chips)),
            dma((PARTS, chips)),
            dma((PARTS, chips)),
            dma((PARTS, chips)),
            dma((PARTS, chips)),
            dma((PARTS, chips)),
            dma((PARTS, 2, half_ring)),
            dma((PARTS, 2, half_ring)),
        ],
        compiler_params=pltpu.CompilerParams(
            collective_id=0, has_side_effects=True, vmem_limit_bytes=64 * 1024 * 1024 - 65536
        ),
    )(routing, task_ids, tokens, gate_weight, w_in, w_out)


def solution(mesh):
    placed = (
        P(("dp", "expert"), None),
        P("dp"),
        P("dp", None),
        P(),
        P("expert", None, "dp"),
        P("expert", "dp", None),
    )
    return jax.shard_map(
        shards, mesh=mesh, in_specs=placed, out_specs=P(("dp", "expert"), None), check_vma=False
    )
```

profile of v0, /device:TPU:0, one launch (start us, length us, event | category | flops | bytes accessed | tf_op | source)
XLA Modules:
  0.0 87.4 jit_solution(8353351781135445402)
XLA Ops:
  0.0 1.3 %copy.7.routing = s32[8,2]{1,0:T(8,128)} copy(s32[8,2]{0,1:T(2,128)} %param.8) | data formatting | bytes 128 | tf_op args[2]
  1.3 1.7 %copy.8.gate_weight = bf16[1024,48]{1,0:T(8,128)(2,1)} copy(bf16[1024,48]{0,1:T(8,128)(2,1)} %param.9) | data formatting | bytes 196608 | tf_op args[3]
  3.1 82.7 %shard_map.64 = bf16[128,1024]{1,0:T(8,128)(2,1)} custom-call(s32[8,2]{1,0:T(8,128)} %copy.7.routing, s32[8]{0:T(128)} %tasks.1, bf16[128,1024]{1,0:T(8,128)(2,1)} %tokens.1, bf16[1024,48]{1,0:T(8,128)(2,1)} %copy.8.gate_weight, bf16[1,1024,1024]{2,1,0:T(8,128)(2,1)} %w_in_hbm.1, bf16[1,1024,1024]{2,1,0:T(8,128)(2,1)} %w_out_hbm.1), custom_call_target="tpu_custom_call" | custom-call | tf_op jit(solution)/shard_map/pallas_call | solution.py:304
  85.7 1.7 %copy.10 = bf16[128,1024]{1,0:T(8,128)(2,1)} copy(bf16[128,1024]{1,0:T(8,128)(2,1)} %shard_map.64) | data formatting | bytes 524288
where the time goes:
time: 87.6 us; the launch traced here: 87.4 us
  Pallas kernels  82.7 us (94%)
  local copies, waits for them, and re-layouts  4.74 us (5%)
    pallas_call x1, Pallas kernels, shards(): pl.pallas_call(functools.partial(kernel, n, n_dp, capacity), out_shape=ja...  82.7 us
    unnamed x3, local copies, waits for them, and re-layouts  4.74 us

commit v1 on v0

v1 whole, which is shorter than its diff:
```python
import functools

import jax
import jax.numpy as jnp
from jax import lax
from jax.experimental import pallas as pl
from jax.experimental.pallas import tpu as pltpu
from jax.sharding import PartitionSpec as P

BLK = 128
ROWS = 16
TILE = 512
MESH = pl.DeviceIdType.MESH
START = {"y": 5.0, "x": 9.0, "relay": 13.2, "expert": 14.4, "back": 16.7, "gate": 20.8, "share": 25.0, "out": 30.0}
STEP = {"y": 2.8, "x": 2.8, "relay": 2.8, "expert": 2.8, "back": 3.5, "gate": 3.5, "share": 3.5, "out": 3.5}


def gelu(x):
    return 0.5 * x * (1.0 + jnp.tanh(0.7978845608028654 * (x + 0.044715 * (x * x * x))))


def kernel(
    n, n_dp, capacity,
    routing, tasks, tokens_hbm, gate_hbm, w_in_hbm, w_out_hbm, out_hbm,
    tokens, gate_weight, w_in, w_out, line, picked, given, cols, hidden, acc, pout, pin, xs, xr, gated,
    weights, shares, landed, result,
    ld, zs, zr, ys, yr, x_s, x_r, b_s, b_r, p_s, p_r, q_s, q_r, v_s, v_r, u_s, u_r, o_s,
):
    d_model = tokens.shape[1]
    parts = BLK // ROWS
    chips = n_dp // 2
    reach = n // 2
    wide = capacity * ROWS
    me = lax.axis_index("expert")
    my_dp = lax.axis_index("dp")
    my_x, my_core = my_dp // 2, my_dp % 2
    at, row = me // 2, me % 2
    other = me + 1 - 2 * row
    pair = {"expert": other}
    sibling = {"dp": my_x * 2 + 1 - my_core}

    def peer(j):
        return {"expert": ((at + j) % reach) * 2 + row}

    def chip(k):
        return {"dp": ((my_x + k) % chips) * 2 + my_core}

    loads = [
        pltpu.make_async_copy(tokens_hbm, tokens, ld.at[0]),
        pltpu.make_async_copy(w_in_hbm.at[0], w_in, ld.at[1]),
        pltpu.make_async_copy(w_out_hbm.at[0], w_out, ld.at[2]),
        pltpu.make_async_copy(gate_hbm, gate_weight, ld.at[3]),
    ]
    for load in loads:
        load.start()

    barrier = pltpu.get_barrier_semaphore()
    partners = [peer(j) for j in range(1, reach)] + [pair, sibling] + [chip(k) for k in range(1, chips)]
    for partner in partners:
        pl.semaphore_signal(barrier, inc=1, device_id=partner, device_id_type=MESH)
    pl.semaphore_wait(barrier, len(partners))

    def remote(src, dst, send, recv, target):
        return pltpu.make_async_remote_copy(
            src_ref=src, dst_ref=dst, send_sem=send, recv_sem=recv,
            device_id=target, device_id_type=MESH,
        )

    sent = []

    def go(copy):
        copy.start()
        sent.append(copy)

    def span(c):
        return slice(c * ROWS, (c + 1) * ROWS)

    def z_copy(c, j):
        return remote(
            tokens.at[pl.ds(c * ROWS, ROWS)], line[c].at[reach - j], zs.at[c, j], zr.at[c, reach - j], peer(j)
        )

    loads[0].wait()
    for c in range(parts):
        for j in range(1, reach):
            go(z_copy(c, j))

    def ranks(expert):
        hits, before, count = [], [], 0
        for m in range(n):
            hit = jnp.where(routing[0, m] == expert, 1, 0) + jnp.where(routing[1, m] == expert, 1, 0)
            hits.append(hit)
            before.append(count)
            count = count + hit
        return hits, before

    def rel(m):
        return (m // 2 + reach - at) % reach

    hits, before = ranks(me)
    theirs, theirs_before = ranks(other)

    def within(taken, member):
        order, count = [], 0
        for m in range(n):
            keep = taken[m] * jnp.where(m % 2 == member, 1, 0)
            order.append((keep, count))
            count = count + keep
        return order

    give = within(theirs, row)
    take = within(hits, 1 - row)
    give_at, slot_at, slot_other, slot_task, slot_valid = [], [], [], [], []
    for slot in range(capacity):
        place = 0
        for m in range(n):
            keep, count = give[m]
            place = place + keep * jnp.where(count == slot, 1, 0) * rel(m)
        give_at.append(jnp.clip(place, 0, reach - 1))
        place, against, task, valid = 0, 0, 0, 0
        for m in range(n):
            here = hits[m] * jnp.where(before[m] == slot, 1, 0)
            near = jnp.where(m % 2 == row, 1, 0)
            place = place + here * (near * rel(m) + (1 - near) * (reach + take[m][1]))
            against = against + here * (routing[0, m] + routing[1, m] - me)
            task = task + here * tasks[m]
            valid = valid + here
        slot_at.append(jnp.clip(place, 0, reach + capacity - 1))
        slot_other.append(against)
        slot_task.append(task)
        slot_valid.append(valid)

    def slot_of(taken, earlier, j, base):
        e = ((at + j) % reach) * 2 + row
        place = 0
        for m in range(n):
            here = taken[m] * jnp.where(m == e, 1, 0)
            place = place + here * (base + earlier[m] - 2 * capacity)
        return jnp.clip(place + 2 * capacity, 0, 2 * capacity)

    mine_for = [slot_of(hits, before, j, 0) for j in range(reach)]
    pair_for = [slot_of(theirs, theirs_before, j, capacity) for j in range(reach)]

    def y_copy(c):
        return remote(picked.at[c], given.at[c], ys.at[c], yr.at[c], pair)

    def x_copy(c, k):
        return remote(
            cols.at[c, 0, 0], cols.at[c, chips - k, 0], x_s.at[c, k], x_r.at[c, chips - k], chip(k)
        )

    def x_recv(c, k):
        return remote(
            cols.at[c, 0, 0], cols.at[c, k, 0], x_s.at[c, chips - k], x_r.at[c, k], chip(chips - k)
        )

    def b_copy(c, k):
        return remote(cols.at[c, k, 0], cols.at[c, k, 1], b_s.at[c, k], b_r.at[c, k], sibling)

    def p_copy(c, k):
        return remote(pout.at[c, k], pin.at[c, k], p_s.at[c, k], p_r.at[c, k], sibling)

    def q_copy(c, k):
        return remote(xs.at[c, k], xr.at[c, chips - k], q_s.at[c, k], q_r.at[c, chips - k], chip(k))

    def q_recv(c, k):
        return remote(xs.at[c, chips - k], xr.at[c, k], q_s.at[c, chips - k], q_r.at[c, k], chip(chips - k))

    def v_copy(c):
        return remote(
            gated[c].at[pl.ds(0, capacity)], gated[c].at[pl.ds(capacity, capacity)], v_s.at[c], v_r.at[c], pair
        )

    def u_copy(c, j):
        return remote(shares.at[c, j], landed.at[c, reach - j], u_s.at[c, j], u_r.at[c, reach - j], peer(j))

    def y_stage(c):
        for j in range(1, reach):
            z_copy(c, reach - j).wait_recv()
        line[c][0] = tokens[span(c), :]
        for slot in range(capacity):
            picked[c, slot] = line[c][give_at[slot]]
        go(y_copy(c))

    def x_stage(c):
        y_copy(c).wait_recv()
        line[c][reach:] = given[c]
        for slot in range(capacity):
            cols[c, 0, 0, slot * ROWS : (slot + 1) * ROWS, :] = line[c][slot_at[slot]]
        for k in range(1, chips):
            go(x_copy(c, k))
        go(b_copy(c, 0))
        if c == 0:
            loads[3].wait()
        logits = lax.dot_general(
            cols[c, 0, 0], gate_weight[...], (((1,), (1,)), ((), ())), preferred_element_type=jnp.float32
        )
        column = lax.broadcasted_iota(jnp.int32, (ROWS, logits.shape[1]), 1)
        for slot in range(capacity):
            own = slot_task[slot] * n + me
            against = slot_task[slot] * n + slot_other[slot]
            sign = jnp.where(column == own, 1.0, 0.0) - jnp.where(column == against, 1.0, 0.0)
            gap = jnp.sum(logits[slot * ROWS : (slot + 1) * ROWS] * sign, axis=1, keepdims=True)
            gate = jax.nn.sigmoid(gap) * slot_valid[slot].astype(jnp.float32)
            weights[c, slot * ROWS : (slot + 1) * ROWS, :] = jnp.broadcast_to(gate, (ROWS, 128))

    def relay_stage(c):
        for k in range(1, chips):
            x_recv(c, k).wait_recv()
            go(b_copy(c, k))

    def expert_stage(c):
        if c == 0:
            loads[1].wait()
            loads[2].wait()
        for k in range(chips):
            b_copy(c, k).wait_recv()
        lhs = cols.at[c]
        tall = chips * 2 * wide

        @pl.loop(0, w_in.shape[1] // TILE)
        def _(t):
            where = pl.ds(pl.multiple_of(t * TILE, TILE), TILE)
            x = lhs[...].reshape(tall, d_model)
            y = jnp.dot(x, w_in[:, where], preferred_element_type=jnp.float32)
            hidden[:, where] = gelu(y).astype(jnp.bfloat16)

        @pl.loop(0, d_model // TILE)
        def _(t):
            where = pl.ds(pl.multiple_of(t * TILE, TILE), TILE)
            y = jnp.dot(hidden[...], w_out[:, where], preferred_element_type=jnp.float32)
            for k in range(chips):
                acc[c, k, :, where] = y[2 * k * wide : (2 * k + 1) * wide]
                pout[c, k, :, where] = y[(2 * k + 1) * wide : (2 * k + 2) * wide].astype(jnp.bfloat16)

        for k in range(chips - 1, -1, -1):
            go(p_copy(c, k))

    def back_stage(c):
        for k in range(1, chips):
            p_copy(c, k).wait_recv()
            xs[c, k] = (acc[c, k] + pin[c, k].astype(jnp.float32)).astype(jnp.bfloat16)
            go(q_copy(c, k))

    def gate_stage(c):
        p_copy(c, 0).wait_recv()
        for k in range(1, chips):
            q_recv(c, k).wait_recv()
        for slot in range(capacity):
            rows = slice(slot * ROWS, (slot + 1) * ROWS)
            total = acc[c, 0, rows, :] + pin[c, 0, rows, :].astype(jnp.float32)
            for k in range(1, chips):
                total = total + xr[c, k, rows, :].astype(jnp.float32)
            gated[c][slot] = (weights[c, rows, :1] * total).astype(jnp.bfloat16)
        gated[c][2 * capacity] = jnp.zeros((ROWS, d_model), jnp.bfloat16)
        go(v_copy(c))

    def share(c, j):
        return gated[c][mine_for[j]].astype(jnp.float32) + gated[c][pair_for[j]].astype(jnp.float32)

    def share_stage(c):
        v_copy(c).wait_recv()
        for j in range(1, reach):
            shares[c, j] = share(c, j).astype(jnp.bfloat16)
            go(u_copy(c, j))

    def out_copy(c):
        return pltpu.make_async_copy(result.at[pl.ds(c * ROWS, ROWS)], out_hbm.at[pl.ds(c * ROWS, ROWS)], o_s.at[c])

    def out_stage(c):
        total = share(c, 0)
        for j in range(1, reach):
            u_copy(c, reach - j).wait_recv()
            total = total + landed[c, j].astype(jnp.float32)
        result[span(c), :] = total.astype(jnp.bfloat16)
        out_copy(c).start()

    stages = {
        "y": y_stage, "x": x_stage, "relay": relay_stage, "expert": expert_stage,
        "back": back_stage, "gate": gate_stage, "share": share_stage, "out": out_stage,
    }
    plan = []
    for c in range(parts):
        for name in stages:
            plan.append((START[name] + STEP[name] * c, len(plan), name, c))
    for _, _, name, c in sorted(plan):
        stages[name](c)
    for copy in sent:
        copy.wait_send()
    for c in range(parts):
        out_copy(c).wait()


def shards(tokens, task_ids, routing, gate_weight, w_in, w_out):
    n = lax.axis_size("expert")
    n_dp = lax.axis_size("dp")
    d_model = tokens.shape[1]
    capacity = 2 * (tokens.shape[0] // BLK) + 1
    chips, reach = n_dp // 2, n // 2
    parts = BLK // ROWS
    wide = capacity * ROWS
    bf16 = jnp.bfloat16
    dma = pltpu.SemaphoreType.DMA
    smem = pl.BlockSpec(memory_space=pltpu.SMEM)
    hbm = pl.BlockSpec(memory_space=pl.ANY)
    return pl.pallas_call(
        functools.partial(kernel, n, n_dp, capacity),
        out_shape=jax.ShapeDtypeStruct(tokens.shape, bf16),
        in_specs=[smem, smem, hbm, hbm, hbm, hbm],
        out_specs=hbm,
        scratch_shapes=[
            pltpu.VMEM(tokens.shape, bf16),
            pltpu.VMEM(gate_weight.shape[::-1], bf16),
            pltpu.VMEM(w_in.shape[1:], bf16),
            pltpu.VMEM(w_out.shape[1:], bf16),
            [pltpu.VMEM((reach + capacity, ROWS, d_model), bf16) for _ in range(parts)],
            pltpu.VMEM((parts, capacity, ROWS, d_model), bf16),
            pltpu.VMEM((parts, capacity, ROWS, d_model), bf16),
            pltpu.VMEM((parts, chips, 2, wide, d_model), bf16),
            pltpu.VMEM((chips * 2 * wide, w_in.shape[2]), bf16),
            pltpu.VMEM((parts, chips, wide, d_model), jnp.float32),
            pltpu.VMEM((parts, chips, wide, d_model), bf16),
            pltpu.VMEM((parts, chips, wide, d_model), bf16),
            pltpu.VMEM((parts, chips, wide, d_model), bf16),
            pltpu.VMEM((parts, chips, wide, d_model), bf16),
            [pltpu.VMEM((2 * capacity + 1, ROWS, d_model), bf16) for _ in range(parts)],
            pltpu.VMEM((parts, wide, 128), jnp.float32),
            pltpu.VMEM((parts, reach, ROWS, d_model), bf16),
            pltpu.VMEM((parts, reach, ROWS, d_model), bf16),
            pltpu.VMEM(tokens.shape, bf16),
            dma((4,)),
            dma((parts, reach)),
            dma((parts, reach)),
            dma((parts,)),
            dma((parts,)),
            dma((parts, chips)),
            dma((parts, chips)),
            dma((parts, chips)),
            dma((parts, chips)),
            dma((parts, chips)),
            dma((parts, chips)),
            dma((parts, chips)),
            dma((parts, chips)),
            dma((parts,)),
            dma((parts,)),
            dma((parts, reach)),
            dma((parts, reach)),
            dma((parts,)),
        ],
        compiler_params=pltpu.CompilerParams(
            collective_id=0, has_side_effects=True, vmem_limit_bytes=64 * 1024 * 1024 - 65536
        ),
    )(routing.T, task_ids, tokens, gate_weight.T, w_in, w_out)


def solution(mesh):
    placed = (
        P(("dp", "expert"), None),
        P("dp"),
        P("dp", None),
        P(),
        P("expert", None, "dp"),
        P("expert", "dp", None),
    )
    return jax.shard_map(
        shards, mesh=mesh, in_specs=placed, out_specs=P(("dp", "expert"), None), check_vma=False
    )
```

time: 87.6 us -> 76.7 us (0.88)
  Pallas kernels: 82.7 us -> 74.8 us
  local copies, waits for them, and re-layouts: 4.74 us -> 1.67 us
    pallas_call x1, Pallas kernels: 82.7 us -> 74.8 us  [shards(): pl.pallas_call(functools.partial(kernel, n, n_dp, capacity), out_shape=ja...]
    unnamed x3 -> x1, local copies, waits for them, and re-layouts: 4.74 us -> 1.67 us
where the time goes in v1:
time: 76.7 us; the launch traced here: 76.5 us
  Pallas kernels  74.8 us (98%)
  local copies, waits for them, and re-layouts  1.67 us (2%)
    pallas_call x1, Pallas kernels, shards(): pl.pallas_call(functools.partial(kernel, n, n_dp, capacity), out_shape=ja...  74.8 us
    unnamed x1, local copies, waits for them, and re-layouts  1.67 us

profile of v1, /device:TPU:0, one launch (start us, length us, event | category | flops | bytes accessed | tf_op | source)
XLA Modules:
  0.0 76.5 jit_solution(5585937935439372247)
XLA Ops:
  0.0 74.8 %shard_map.64 = bf16[128,1024]{1,0:T(8,128)(2,1)} custom-call(s32[2,8]{1,0:T(2,128)} %bitcast.3, s32[8]{0:T(128)} %tasks.1, bf16[128,1024]{1,0:T(8,128)(2,1)} %tokens_hbm.1, bf16[48,1024]{1,0:T(8,128)(2,1)} %bitcast.2, bf16[1,1024,1024]{2,1,0:T(8,128)(2,1)} %w_in_hbm.1, bf16[1,1024,1024]{2,1,0:T(8,128)(2,1)} %w_out_hbm.1), custom_call_target="tpu_custom_call" | custom-call | tf_op jit(solution)/shard_map/pallas_call | solution.py:306
  74.8 1.7 %copy.8 = bf16[128,1024]{1,0:T(8,128)(2,1)} copy(bf16[128,1024]{1,0:T(8,128)(2,1)} %shard_map.64) | data formatting | bytes 524288

commit v2 on v1

v2 whole, which is shorter than its diff:
```python
import functools

import jax
import jax.numpy as jnp
from jax import lax
from jax.experimental import pallas as pl
from jax.experimental.pallas import tpu as pltpu
from jax.sharding import PartitionSpec as P

BLK = 128
ROWS = 16
PIECES = 2
MESH = pl.DeviceIdType.MESH
LAGS = {
    "z": -7.0, "zf": -2.0, "y": -0.8, "x": 1.2, "relay": 2.7, "expert": 3.4, "back": 4.6, "gate": 6.4,
    "share": 8.5, "sf": 10.5, "out": 13.5,
}


def gelu(x):
    return 0.5 * x * (1.0 + jnp.tanh(0.7978845608028654 * (x + 0.044715 * (x * x * x))))


def kernel(
    n, n_dp, capacity, pieces,
    routing_hbm, tasks_hbm, tokens_hbm, gate_hbm, w_in_hbm, w_out_hbm, out_hbm,
    routing, tasks, tokens, gate_weight, w_in, w_out, line, picked, given, cols, hidden, acc, pout, pin, xs, xr,
    gated, weights, shares, passed, landed, result,
    ld, far, zs, zr, ys, yr, x_s, x_r, b_s, b_r, p_s, p_r, q_s, q_r, v_s, v_r, u_s, u_r, f_r, o_s,
):
    d_model = tokens.shape[1]
    width = d_model // pieces
    parts = BLK // ROWS
    chips = n_dp // 2
    reach = n // 2
    wide = capacity * ROWS
    hops = min(2, reach - 1)
    me = lax.axis_index("expert")
    my_dp = lax.axis_index("dp")
    my_x, my_core = my_dp // 2, my_dp % 2
    at, row = me // 2, me % 2
    other = me + 1 - 2 * row
    pair = {"expert": other}
    sibling = {"dp": my_x * 2 + 1 - my_core}

    def along(way, hop):
        return {"expert": (at + hop if way == 0 else at - hop) * 2 + row}

    def ahead(way, hop):
        return at + hop < reach if way == 0 else at >= hop

    def behind(way, hop):
        return ahead(1 - way, hop)

    def chip(k):
        return {"dp": ((my_x + k) % chips) * 2 + my_core}

    loads = [
        pltpu.make_async_copy(tokens_hbm, tokens, ld.at[0]),
        pltpu.make_async_copy(routing_hbm, routing, ld.at[4]),
        pltpu.make_async_copy(tasks_hbm, tasks, ld.at[5]),
        pltpu.make_async_copy(gate_hbm, gate_weight, ld.at[3]),
        pltpu.make_async_copy(w_in_hbm.at[0], w_in, ld.at[1]),
        pltpu.make_async_copy(w_out_hbm.at[0], w_out, ld.at[2]),
    ]
    for load in loads[:3]:
        load.start()

    barrier = pltpu.get_barrier_semaphore()
    for way in range(2):

        @pl.when(ahead(way, 1))
        def _():
            pl.semaphore_signal(barrier, inc=1, device_id=along(way, 1), device_id_type=MESH)

    partners = [pair, sibling] + [chip(k) for k in range(1, chips)]
    for partner in partners:
        pl.semaphore_signal(barrier, inc=1, device_id=partner, device_id_type=MESH)
    for load in loads[3:]:
        load.start()
    ends = jnp.where(at == 0, 1, 0) + jnp.where(at == reach - 1, 1, 0)
    pl.semaphore_wait(barrier, len(partners) + 2 - ends)

    def remote(src, dst, send, recv, target):
        return pltpu.make_async_remote_copy(
            src_ref=src, dst_ref=dst, send_sem=send, recv_sem=recv,
            device_id=target, device_id_type=MESH,
        )

    sent = []

    def go(copy):
        copy.start()
        sent.append((None, copy))

    def go_if(cond, make):
        @pl.when(cond)
        def _():
            make().start()

        sent.append((cond, make))

    def wait_if(cond, make):
        @pl.when(cond)
        def _():
            make().wait_recv()

    def where_of(i):
        c, s = i // pieces, i % pieces
        return c, s, slice(c * ROWS, (c + 1) * ROWS), slice(s * width, (s + 1) * width)

    def place(way, d):
        return reach - d if way == 0 else d

    def z_copy(i, way, hop):
        c, s, _, _ = where_of(i)
        src = tokens.at[pl.ds(c * ROWS, ROWS), pl.ds(s * width, width)]
        return remote(src, line[i].at[place(way, hop)], zs.at[i, way, hop], zr.at[i, way, hop], along(way, hop))

    def zf_copy(i, way, d):
        return remote(
            line[i].at[place(way, d)], line[i].at[place(way, d + 1)],
            zs.at[i, way, d + 1], zr.at[i, way, d + 1], along(way, 1),
        )

    def z_wait(i, d):
        for way in range(2):
            wait_if(behind(way, d), lambda: z_copy(i, way, 1) if d == 1 else zf_copy(i, way, d - 1))

    def z_stage(i, which):
        for hop in which:
            for way in range(2):
                go_if(ahead(way, hop), functools.partial(z_copy, i, way, hop))

    def zf_stage(i):
        for d in range(2, reach - 1):
            z_wait(i, d)
            for way in range(2):
                go_if(jnp.logical_and(behind(way, d), ahead(way, 1)), functools.partial(zf_copy, i, way, d))

    loads[0].wait()
    z_stage(0, [1])
    if hops > 1:
        for way in range(2):

            @pl.when(jnp.logical_and(ahead(way, 1), behind(way, 1)))
            def _():
                pl.semaphore_signal(far.at[way], inc=1, device_id=along(way, 1), device_id_type=MESH)

        for way in range(2):

            @pl.when(behind(way, 2))
            def _():
                pl.semaphore_wait(far.at[way], 1)

        z_stage(0, [2])
    every = list(range(1, hops + 1))
    ready = max(1, int(-LAGS["z"]) - 2)
    for i in range(1, ready):
        z_stage(i, every)

    loads[1].wait()
    loads[2].wait()

    def ranks(expert):
        hits, before, count = [], [], 0
        for m in range(n):
            hit = jnp.where(routing[0, m] == expert, 1, 0) + jnp.where(routing[1, m] == expert, 1, 0)
            hits.append(hit)
            before.append(count)
            count = count + hit
        return hits, before

    def rel(m):
        return (m // 2 + reach - at) % reach

    hits, before = ranks(me)
    theirs, theirs_before = ranks(other)

    def within(taken, member):
        order, count = [], 0
        for m in range(n):
            keep = taken[m] * jnp.where(m % 2 == member, 1, 0)
            order.append((keep, count))
            count = count + keep
        return order

    give = within(theirs, row)
    take = within(hits, 1 - row)
    give_at, slot_at, slot_other, slot_task, slot_valid = [], [], [], [], []
    for slot in range(capacity):
        spot = 0
        for m in range(n):
            keep, count = give[m]
            spot = spot + keep * jnp.where(count == slot, 1, 0) * rel(m)
        give_at.append(jnp.clip(spot, 0, reach - 1))
        spot, against, task, valid = 0, 0, 0, 0
        for m in range(n):
            here = hits[m] * jnp.where(before[m] == slot, 1, 0)
            near = jnp.where(m % 2 == row, 1, 0)
            spot = spot + here * (near * rel(m) + (1 - near) * (reach + take[m][1]))
            against = against + here * (routing[0, m] + routing[1, m] - me)
            task = task + here * tasks[m]
            valid = valid + here
        slot_at.append(jnp.clip(spot, 0, reach + capacity - 1))
        slot_other.append(against)
        slot_task.append(task)
        slot_valid.append(valid)

    def slot_of(taken, earlier, j, base):
        e = ((at + j) % reach) * 2 + row
        spot = 0
        for m in range(n):
            here = taken[m] * jnp.where(m == e, 1, 0)
            spot = spot + here * (base + earlier[m] - 2 * capacity)
        return jnp.clip(spot + 2 * capacity, 0, 2 * capacity)

    mine_for = [slot_of(hits, before, j, 0) for j in range(reach)]
    pair_for = [slot_of(theirs, theirs_before, j, capacity) for j in range(reach)]

    def y_copy(i):
        return remote(picked.at[i], given.at[i], ys.at[i], yr.at[i], pair)

    def x_copy(i, k):
        return remote(
            cols.at[i, 0, 0], cols.at[i, chips - k, 0], x_s.at[i, k], x_r.at[i, chips - k], chip(k)
        )

    def x_recv(i, k):
        return remote(
            cols.at[i, 0, 0], cols.at[i, k, 0], x_s.at[i, chips - k], x_r.at[i, k], chip(chips - k)
        )

    def b_copy(i, k):
        return remote(cols.at[i, k, 0], cols.at[i, k, 1], b_s.at[i, k], b_r.at[i, k], sibling)

    def p_copy(i, k):
        return remote(pout.at[i, k], pin.at[i, k], p_s.at[i, k], p_r.at[i, k], sibling)

    def q_copy(i, k):
        return remote(xs.at[i, k], xr.at[i, chips - k], q_s.at[i, k], q_r.at[i, chips - k], chip(k))

    def q_recv(i, k):
        return remote(xs.at[i, chips - k], xr.at[i, k], q_s.at[i, chips - k], q_r.at[i, k], chip(chips - k))

    def v_copy(i):
        return remote(
            gated[i].at[pl.ds(0, capacity)], gated[i].at[pl.ds(capacity, capacity)], v_s.at[i], v_r.at[i], pair
        )

    def u_copy(i, way, j):
        if j > hops:
            return remote(
                shares.at[i, way, j], passed.at[i, way, j - 1],
                u_s.at[i, way, j], f_r.at[i, way, j - 1], along(way, 1),
            )
        return remote(
            shares.at[i, way, j], landed.at[i, way, j], u_s.at[i, way, j], u_r.at[i, way, j], along(way, j)
        )

    def y_stage(i):
        c, s, rows, part = where_of(i)
        for d in sorted({1, reach - 1}):
            z_wait(i, d)
        line[i][0] = tokens[rows, part]
        for slot in range(capacity):
            picked[i, slot] = line[i][give_at[slot]]
        go(y_copy(i))

    def x_stage(i):
        y_copy(i).wait_recv()
        line[i][reach:] = given[i]
        for slot in range(capacity):
            cols[i, 0, 0, slot * ROWS : (slot + 1) * ROWS, :] = line[i][slot_at[slot]]
        for k in range(1, chips):
            go(x_copy(i, k))
        go(b_copy(i, 0))
        if i == 0:
            loads[3].wait()
        if i % pieces == pieces - 1:
            gates(i // pieces)

    def whole(c, *index):
        return jnp.concatenate([cols[(c * pieces + s, *index)] for s in range(pieces)], axis=-1)

    def gates(c):
        logits = lax.dot_general(
            whole(c, 0, 0), gate_weight[...], (((1,), (1,)), ((), ())), preferred_element_type=jnp.float32
        )
        column = lax.broadcasted_iota(jnp.int32, (ROWS, logits.shape[1]), 1)
        for slot in range(capacity):
            own = slot_task[slot] * n + me
            against = slot_task[slot] * n + slot_other[slot]
            sign = jnp.where(column == own, 1.0, 0.0) - jnp.where(column == against, 1.0, 0.0)
            gap = jnp.sum(logits[slot * ROWS : (slot + 1) * ROWS] * sign, axis=1, keepdims=True)
            gate = jax.nn.sigmoid(gap) * slot_valid[slot].astype(jnp.float32)
            weights[c, slot * ROWS : (slot + 1) * ROWS, :] = jnp.broadcast_to(gate, (ROWS, 128))

    def relay_stage(i):
        for k in range(1, chips):
            x_recv(i, k).wait_recv()
            go(b_copy(i, k))

    def expert_stage(i):
        c = i // pieces
        if c == 0:
            loads[4].wait()
            loads[5].wait()
        for s in range(pieces):
            for k in range(chips):
                b_copy(c * pieces + s, k).wait_recv()
        tall = chips * 2 * wide
        x = whole(c).reshape(tall, d_model)
        y = jnp.dot(x, w_in[...], preferred_element_type=jnp.float32)
        hidden[...] = gelu(y).astype(jnp.bfloat16)
        for s in range(pieces):
            u = c * pieces + s
            y = jnp.dot(hidden[...], w_out[:, s * width : (s + 1) * width], preferred_element_type=jnp.float32)
            for k in range(chips - 1, -1, -1):
                acc[u, k] = y[2 * k * wide : (2 * k + 1) * wide]
                pout[u, k] = y[(2 * k + 1) * wide : (2 * k + 2) * wide].astype(jnp.bfloat16)
                go(p_copy(u, k))

    def back_stage(i):
        for k in range(1, chips):
            p_copy(i, k).wait_recv()
            xs[i, k] = (acc[i, k] + pin[i, k].astype(jnp.float32)).astype(jnp.bfloat16)
            go(q_copy(i, k))

    def gate_stage(i):
        p_copy(i, 0).wait_recv()
        for k in range(1, chips):
            q_recv(i, k).wait_recv()
        for slot in range(capacity):
            rows = slice(slot * ROWS, (slot + 1) * ROWS)
            total = acc[i, 0, rows, :] + pin[i, 0, rows, :].astype(jnp.float32)
            for k in range(1, chips):
                total = total + xr[i, k, rows, :].astype(jnp.float32)
            gated[i][slot] = (weights[i // pieces, rows, :1] * total).astype(jnp.bfloat16)
        gated[i][2 * capacity] = jnp.zeros((ROWS, width), jnp.bfloat16)
        go(v_copy(i))

    def share(i, j):
        return gated[i][mine_for[j]].astype(jnp.float32) + gated[i][pair_for[j]].astype(jnp.float32)

    def share_stage(i):
        v_copy(i).wait_recv()
        for j in range(reach - 1, 0, -1):
            for way in range(2):
                shares[i, way, j] = share(i, j if way == 0 else reach - j).astype(jnp.bfloat16)
                cond = ahead(way, j)
                if j >= hops and j > 1:
                    cond = jnp.logical_and(cond, jnp.logical_not(behind(way, 1)))
                go_if(cond, functools.partial(u_copy, i, way, j))

    def sf_stage(i):
        for j in range(reach - 2, 1, -1):
            for way in range(2):
                cond = jnp.logical_and(ahead(way, j), behind(way, 1))

                @pl.when(cond)
                def _():
                    u_copy(i, way, j + 1).wait_recv()
                    total = shares[i, way, j].astype(jnp.float32) + passed[i, way, j].astype(jnp.float32)
                    shares[i, way, j] = total.astype(jnp.bfloat16)

                go_if(cond, functools.partial(u_copy, i, way, j))

    def out_copy(i):
        c, s, _, _ = where_of(i)
        spot = (pl.ds(c * ROWS, ROWS), pl.ds(s * width, width))
        return pltpu.make_async_copy(result.at[spot], out_hbm.at[spot], o_s.at[i])

    def out_stage(i):
        c, s, rows, part = where_of(i)
        total = share(i, 0)
        for j in range(1, hops + 1):
            for way in range(2):
                wait_if(behind(way, j), functools.partial(u_copy, i, way, j))
                total = total + jnp.where(behind(way, j), landed[i, way, j].astype(jnp.float32), 0.0)
        result[rows, part] = total.astype(jnp.bfloat16)
        out_copy(i).start()

    stages = {
        "z": lambda i: z_stage(i, every), "zf": zf_stage, "y": y_stage, "x": x_stage, "relay": relay_stage,
        "expert": expert_stage, "back": back_stage, "gate": gate_stage, "share": share_stage, "sf": sf_stage,
        "out": out_stage,
    }
    plan = []
    for i in range(parts * pieces):
        for name in stages:
            if name == "z" and i < ready:
                continue
            if name == "expert" and i % pieces < pieces - 1:
                continue
            plan.append((LAGS[name] + i, len(plan), name, i))
    for _, _, name, i in sorted(plan):
        stages[name](i)
    for cond, copy in sent:
        if cond is None:
            copy.wait_send()
        else:

            @pl.when(cond)
            def _():
                copy().wait_send()

    for i in range(parts * pieces):
        out_copy(i).wait()


def shards(tokens, task_ids, routing, gate_weight, w_in, w_out):
    n = lax.axis_size("expert")
    n_dp = lax.axis_size("dp")
    d_model = tokens.shape[1]
    capacity = 2 * (tokens.shape[0] // BLK) + 1
    chips, reach = n_dp // 2, n // 2
    parts = BLK // ROWS
    pieces = PIECES if reach <= 4 else 1
    units, width = parts * pieces, d_model // pieces
    wide = capacity * ROWS
    bf16 = jnp.bfloat16
    dma = pltpu.SemaphoreType.DMA
    hbm = pl.BlockSpec(memory_space=pl.ANY)

    def vmem(*shape):
        return pltpu.VMEM(shape, bf16)

    return pl.pallas_call(
        functools.partial(kernel, n, n_dp, capacity, pieces),
        out_shape=jax.ShapeDtypeStruct(tokens.shape, bf16),
        in_specs=[hbm] * 6,
        out_specs=hbm,
        scratch_shapes=[
            pltpu.SMEM(routing.shape[::-1], jnp.int32),
            pltpu.SMEM(task_ids.shape, jnp.int32),
            vmem(*tokens.shape),
            vmem(*gate_weight.shape[::-1]),
            vmem(*w_in.shape[1:]),
            vmem(*w_out.shape[1:]),
            [vmem(reach + capacity, ROWS, width) for _ in range(units)],
            vmem(units, capacity, ROWS, width),
            vmem(units, capacity, ROWS, width),
            vmem(units, chips, 2, wide, width),
            vmem(chips * 2 * wide, w_in.shape[2]),
            pltpu.VMEM((units, chips, wide, width), jnp.float32),
            vmem(units, chips, wide, width),
            vmem(units, chips, wide, width),
            vmem(units, chips, wide, width),
            vmem(units, chips, wide, width),
            [vmem(2 * capacity + 1, ROWS, width) for _ in range(units)],
            pltpu.VMEM((parts, wide, 128), jnp.float32),
            vmem(units, 2, reach, ROWS, width),
            vmem(units, 2, reach, ROWS, width),
            vmem(units, 2, 3, ROWS, width),
            vmem(*tokens.shape),
            dma((6,)),
            pltpu.SemaphoreType.REGULAR((2,)),
            dma((units, 2, reach)),
            dma((units, 2, reach)),
            dma((units,)),
            dma((units,)),
            dma((units, chips)),
            dma((units, chips)),
            dma((units, chips)),
            dma((units, chips)),
            dma((units, chips)),
            dma((units, chips)),
            dma((units, chips)),
            dma((units, chips)),
            dma((units,)),
            dma((units,)),
            dma((units, 2, reach)),
            dma((units, 2, 3)),
            dma((units, 2, reach)),
            dma((units,)),
        ],
        compiler_params=pltpu.CompilerParams(
            collective_id=0, has_side_effects=True, vmem_limit_bytes=64 * 1024 * 1024 - 65536
        ),
    )(routing.T, task_ids, tokens, gate_weight.T, w_in, w_out)


def solution(mesh):
    placed = (
        P(("dp", "expert"), None),
        P("dp"),
        P("dp", None),
        P(),
        P("expert", None, "dp"),
        P("expert", "dp", None),
    )
    return jax.shard_map(
        shards, mesh=mesh, in_specs=placed, out_specs=P(("dp", "expert"), None), check_vma=False
    )
```

time: 76.7 us -> 83.8 us (1.093)
  Pallas kernels: 74.8 us -> 82 us
    pallas_call x1, Pallas kernels: 74.8 us -> 82 us  [shards(): pl.pallas_call(functools.partial(kernel, n, n_dp, capacity, pieces), out_...]
where the time goes in v2:
time: 83.8 us; the launch traced here: 83.7 us
  Pallas kernels  82 us (98%)
  local copies, waits for them, and re-layouts  1.67 us (2%)
    pallas_call x1, Pallas kernels, shards(): pl.pallas_call(functools.partial(kernel, n, n_dp, capacity, pieces), out_...  82 us

profile of v2, /device:TPU:0, one launch (start us, length us, event | category | flops | bytes accessed | tf_op | source)
XLA Modules:
  0.0 83.7 jit_solution(9866087654443057818)
XLA Ops:
  0.0 82.0 %shard_map.64 = bf16[128,1024]{1,0:T(8,128)(2,1)} custom-call(s32[2,8]{1,0:T(2,128)} %bitcast.3, s32[8]{0:T(128)} %tasks_hbm.1, bf16[128,1024]{1,0:T(8,128)(2,1)} %tokens_hbm.1, bf16[48,1024]{1,0:T(8,128)(2,1)} %bitcast.2, bf16[1,1024,1024]{2,1,0:T(8,128)(2,1)} %w_in_hbm.1, bf16[1,1024,1024]{2,1,0:T(8,128)(2,1)} %w_out_hbm.1), custom_call_target="tpu_custom_call" | custom-call | tf_op jit(solution)/shard_map/pallas_call | solution.py:429
  82.0 1.7 %copy.8 = bf16[128,1024]{1,0:T(8,128)(2,1)} copy(bf16[128,1024]{1,0:T(8,128)(2,1)} %shard_map.64) | data formatting | bytes 524288

commit v3 on v1

--- a/solution.py
+++ b/solution.py
@@ -9,10 +9,8 @@
 
 BLK = 128
 ROWS = 16
-TILE = 512
 MESH = pl.DeviceIdType.MESH
-START = {"y": 5.0, "x": 9.0, "relay": 13.2, "expert": 14.4, "back": 16.7, "gate": 20.8, "share": 25.0, "out": 30.0}
-STEP = {"y": 2.8, "x": 2.8, "relay": 2.8, "expert": 2.8, "back": 3.5, "gate": 3.5, "share": 3.5, "out": 3.5}
+LAGS = {"y": 0, "x": 1.25, "relay": 2.5, "expert": 2.9, "back": 3.6, "gate": 4.9, "share": 6.2, "out": 7.9}
 
 
 def gelu(x):
@@ -21,8 +19,8 @@
 
 def kernel(
     n, n_dp, capacity,
-    routing, tasks, tokens_hbm, gate_hbm, w_in_hbm, w_out_hbm, out_hbm,
-    tokens, gate_weight, w_in, w_out, line, picked, given, cols, hidden, acc, pout, pin, xs, xr, gated,
+    routing_hbm, tasks_hbm, tokens_hbm, gate_hbm, w_in_hbm, w_out_hbm, out_hbm,
+    routing, tasks, tokens, gate_weight, w_in, w_out, line, picked, given, cols, hidden, acc, pout, pin, xs, xr, gated,
     weights, shares, landed, result,
     ld, zs, zr, ys, yr, x_s, x_r, b_s, b_r, p_s, p_r, q_s, q_r, v_s, v_r, u_s, u_r, o_s,
 ):
@@ -50,8 +48,10 @@
         pltpu.make_async_copy(w_in_hbm.at[0], w_in, ld.at[1]),
         pltpu.make_async_copy(w_out_hbm.at[0], w_out, ld.at[2]),
         pltpu.make_async_copy(gate_hbm, gate_weight, ld.at[3]),
+        pltpu.make_async_copy(routing_hbm, routing, ld.at[4]),
+        pltpu.make_async_copy(tasks_hbm, tasks, ld.at[5]),
     ]
-    for load in loads:
+    for load in [loads[0]] + loads[4:] + loads[1:4]:
         load.start()
 
     barrier = pltpu.get_barrier_semaphore()
@@ -84,6 +84,9 @@
     for c in range(parts):
         for j in range(1, reach):
             go(z_copy(c, j))
+
+    loads[4].wait()
+    loads[5].wait()
 
     def ranks(expert):
         hits, before, count = [], [], 0
@@ -218,22 +221,13 @@
         lhs = cols.at[c]
         tall = chips * 2 * wide
 
-        @pl.loop(0, w_in.shape[1] // TILE)
-        def _(t):
-            where = pl.ds(pl.multiple_of(t * TILE, TILE), TILE)
-            x = lhs[...].reshape(tall, d_model)
-            y = jnp.dot(x, w_in[:, where], preferred_element_type=jnp.float32)
-            hidden[:, where] = gelu(y).astype(jnp.bfloat16)
-
-        @pl.loop(0, d_model // TILE)
-        def _(t):
-            where = pl.ds(pl.multiple_of(t * TILE, TILE), TILE)
-            y = jnp.dot(hidden[...], w_out[:, where], preferred_element_type=jnp.float32)
-            for k in range(chips):
-                acc[c, k, :, where] = y[2 * k * wide : (2 * k + 1) * wide]
-                pout[c, k, :, where] = y[(2 * k + 1) * wide : (2 * k + 2) * wide].astype(jnp.bfloat16)
-
+        x = lhs[...].reshape(tall, d_model)
+        y = jnp.dot(x, w_in[...], preferred_element_type=jnp.float32)
+        hidden[...] = gelu(y).astype(jnp.bfloat16)
+        y = jnp.dot(hidden[...], w_out[...], preferred_element_type=jnp.float32)
         for k in range(chips - 1, -1, -1):
+            acc[c, k] = y[2 * k * wide : (2 * k + 1) * wide]
+            pout[c, k] = y[(2 * k + 1) * wide : (2 * k + 2) * wide].astype(jnp.bfloat16)
             go(p_copy(c, k))
 
     def back_stage(c):
@@ -282,7 +276,7 @@
     plan = []
     for c in range(parts):
         for name in stages:
-            plan.append((START[name] + STEP[name] * c, len(plan), name, c))
+            plan.append((LAGS[name] + c, len(plan), name, c))
     for _, _, name, c in sorted(plan):
         stages[name](c)
     for copy in sent:
@@ -301,14 +295,15 @@
     wide = capacity * ROWS
     bf16 = jnp.bfloat16
     dma = pltpu.SemaphoreType.DMA
-    smem = pl.BlockSpec(memory_space=pltpu.SMEM)
     hbm = pl.BlockSpec(memory_space=pl.ANY)
     return pl.pallas_call(
         functools.partial(kernel, n, n_dp, capacity),
         out_shape=jax.ShapeDtypeStruct(tokens.shape, bf16),
-        in_specs=[smem, smem, hbm, hbm, hbm, hbm],
+        in_specs=[hbm] * 6,
         out_specs=hbm,
         scratch_shapes=[
+            pltpu.SMEM(routing.shape[::-1], jnp.int32),
+            pltpu.SMEM(task_ids.shape, jnp.int32),
             pltpu.VMEM(tokens.shape, bf16),
             pltpu.VMEM(gate_weight.shape[::-1], bf16),
             pltpu.VMEM(w_in.shape[1:], bf16),
@@ -328,7 +323,7 @@
             pltpu.VMEM((parts, reach, ROWS, d_model), bf16),
             pltpu.VMEM((parts, reach, ROWS, d_model), bf16),
             pltpu.VMEM(tokens.shape, bf16),
-            dma((4,)),
+            dma((6,)),
             dma((parts, reach)),
             dma((parts, reach)),
             dma((parts,)),

time: 76.7 us -> 70.8 us (0.923)
  Pallas kernels: 74.8 us -> 69 us
    pallas_call x1, Pallas kernels: 74.8 us -> 69 us  [shards(): pl.pallas_call(functools.partial(kernel, n, n_dp, capacity), out_shape=ja...]
where the time goes in v3:
time: 70.8 us; the launch traced here: 70.7 us
  Pallas kernels  69 us (97%)
  local copies, waits for them, and re-layouts  1.67 us (2%)
    pallas_call x1, Pallas kernels, shards(): pl.pallas_call(functools.partial(kernel, n, n_dp, capacity), out_shape=ja...  69 us
    unnamed x1, local copies, waits for them, and re-layouts  1.67 us

profile of v3, /device:TPU:0, one launch (start us, length us, event | category | flops | bytes accessed | tf_op | source)
XLA Modules:
  0.0 70.7 jit_solution(2147485954772701521)
XLA Ops:
  0.0 69.0 %shard_map.64 = bf16[128,1024]{1,0:T(8,128)(2,1)} custom-call(s32[2,8]{1,0:T(2,128)} %bitcast.3, s32[8]{0:T(128)} %tasks_hbm.1, bf16[128,1024]{1,0:T(8,128)(2,1)} %tokens_hbm.1, bf16[48,1024]{1,0:T(8,128)(2,1)} %bitcast.2, bf16[1,1024,1024]{2,1,0:T(8,128)(2,1)} %w_in_hbm.1, bf16[1,1024,1024]{2,1,0:T(8,128)(2,1)} %w_out_hbm.1), custom_call_target="tpu_custom_call" | custom-call | tf_op jit(solution)/shard_map/pallas_call | solution.py:299
  69.0 1.7 %copy.8 = bf16[128,1024]{1,0:T(8,128)(2,1)} copy(bf16[128,1024]{1,0:T(8,128)(2,1)} %shard_map.64) | data formatting | bytes 524288

commit v4 on v3

--- a/solution.py
+++ b/solution.py
@@ -10,7 +10,7 @@
 BLK = 128
 ROWS = 16
 MESH = pl.DeviceIdType.MESH
-LAGS = {"y": 0, "x": 1.25, "relay": 2.5, "expert": 2.9, "back": 3.6, "gate": 4.9, "share": 6.2, "out": 7.9}
+LAGS = {"y": 0, "x": 1.25, "relay": 2.5, "expert": 2.9, "back": 3.6, "gate": 4.9, "share": 6.2, "out": 20}
 
 
 def gelu(x):

time: 70.8 us -> 69.6 us (0.983)
  Pallas kernels: 69 us -> 67.8 us
    pallas_call x1, Pallas kernels: 69 us -> 67.8 us  [shards(): pl.pallas_call(functools.partial(kernel, n, n_dp, capacity), out_shape=ja...]
where the time goes in v4:
time: 69.6 us; the launch traced here: 69.5 us
  Pallas kernels  67.8 us (97%)
  local copies, waits for them, and re-layouts  1.67 us (2%)
    pallas_call x1, Pallas kernels, shards(): pl.pallas_call(functools.partial(kernel, n, n_dp, capacity), out_shape=ja...  67.8 us
    unnamed x1, local copies, waits for them, and re-layouts  1.67 us

profile of v4, /device:TPU:0, one launch (start us, length us, event | category | flops | bytes accessed | tf_op | source)
XLA Modules:
  0.0 69.5 jit_solution(5346704632256958993)
XLA Ops:
  0.0 67.8 %shard_map.64 = bf16[128,1024]{1,0:T(8,128)(2,1)} custom-call(s32[2,8]{1,0:T(2,128)} %bitcast.3, s32[8]{0:T(128)} %tasks_hbm.1, bf16[128,1024]{1,0:T(8,128)(2,1)} %tokens_hbm.1, bf16[48,1024]{1,0:T(8,128)(2,1)} %bitcast.2, bf16[1,1024,1024]{2,1,0:T(8,128)(2,1)} %w_in_hbm.1, bf16[1,1024,1024]{2,1,0:T(8,128)(2,1)} %w_out_hbm.1), custom_call_target="tpu_custom_call" | custom-call | tf_op jit(solution)/shard_map/pallas_call | solution.py:299
  67.8 1.7 %copy.8 = bf16[128,1024]{1,0:T(8,128)(2,1)} copy(bf16[128,1024]{1,0:T(8,128)(2,1)} %shard_map.64) | data formatting | bytes 524288

commit v5 on v4

--- a/solution.py
+++ b/solution.py
@@ -9,6 +9,7 @@
 
 BLK = 128
 ROWS = 16
+STEPS = {"gate": 1.12, "share": 1.12}
 MESH = pl.DeviceIdType.MESH
 LAGS = {"y": 0, "x": 1.25, "relay": 2.5, "expert": 2.9, "back": 3.6, "gate": 4.9, "share": 6.2, "out": 20}
 
@@ -276,7 +277,7 @@
     plan = []
     for c in range(parts):
         for name in stages:
-            plan.append((LAGS[name] + c, len(plan), name, c))
+            plan.append((LAGS[name] + STEPS.get(name, 1.0) * c, len(plan), name, c))
     for _, _, name, c in sorted(plan):
         stages[name](c)
     for copy in sent:

time: 69.6 us -> 69.1 us (level)
  no operation moved by 1% of the time
where the time goes in v5:
time: 69.1 us; the launch traced here: 68.9 us
  Pallas kernels  67.2 us (97%)
  local copies, waits for them, and re-layouts  1.67 us (2%)
    pallas_call x1, Pallas kernels, shards(): pl.pallas_call(functools.partial(kernel, n, n_dp, capacity), out_shape=ja...  67.2 us
    unnamed x1, local copies, waits for them, and re-layouts  1.67 us

profile of v5, /device:TPU:0, one launch (start us, length us, event | category | flops | bytes accessed | tf_op | source)
XLA Modules:
  0.0 68.9 jit_solution(10817355315534741904)
XLA Ops:
  0.0 67.2 %shard_map.64 = bf16[128,1024]{1,0:T(8,128)(2,1)} custom-call(s32[2,8]{1,0:T(2,128)} %bitcast.3, s32[8]{0:T(128)} %tasks_hbm.1, bf16[128,1024]{1,0:T(8,128)(2,1)} %tokens_hbm.1, bf16[48,1024]{1,0:T(8,128)(2,1)} %bitcast.2, bf16[1,1024,1024]{2,1,0:T(8,128)(2,1)} %w_in_hbm.1, bf16[1,1024,1024]{2,1,0:T(8,128)(2,1)} %w_out_hbm.1), custom_call_target="tpu_custom_call" | custom-call | tf_op jit(solution)/shard_map/pallas_call | solution.py:300
  67.3 1.7 %copy.8 = bf16[128,1024]{1,0:T(8,128)(2,1)} copy(bf16[128,1024]{1,0:T(8,128)(2,1)} %shard_map.64) | data formatting | bytes 524288
